TPU v7x, 32 devices: a whole 2x2x4 slice. The times are simulated.
32 devices in a mesh: block: 2 (over z_hi), span: 4 (over y, x), group: 4 (over z_lo, core).
Axes of the slice: x: 2, y: 2, z: 4 (z_hi: 2, z_lo: 2; z = z_hi * 2 + z_lo), core: 2. Of those that a mesh axis runs over, the one named last changes fastest.
Arguments:
- key_rows: bfloat16 [8, 12288, 8, 128], P(None, ('block', 'span'), 'group'), may hold values from -6 to 6
- value_rows: bfloat16 [8, 12288, 8, 128], P(None, ('block', 'span'), 'group'), may hold values from -6 to 6
- turn_angle: float32 [12288, 64], replicated, may hold values from -3.140625 to 3.140625
- key_gain: float32 [128], replicated, may hold values from 0.25 to 1.75
Outputs:
- stored_keys: bfloat16 [8, 8, 128, 12288], P(('block', 'span'), 'group')
- stored_values: bfloat16 [8, 12288, 8, 128], P(('block', 'span'), None, 'group')
- key_scale: float32 [8, 8, 128], P(('block', 'span'), 'group')
All inputs are finite; a program needn't handle non-finite values. Where the computation divides by a largest or mean magnitude, that divisor is 1e-20 or more.
Results may differ from a plain program's by a relative error of at most 0.001.
Values may be sent and summed in bfloat16 or wider, within the bound.
A program may use at most 128 MiB of HBM per device.

v0:
```python
import jax
import jax.numpy as jnp
from jax import lax
from jax.sharding import PartitionSpec as P


def apply_rotary(vectors, angle):
    half = vectors.shape[-1] // 2
    cosine, sine = (jnp.cos(angle)[None, :, None, :], jnp.sin(angle)[None, :, None, :])
    first, second = (vectors[..., :half], vectors[..., half:])
    return jnp.concatenate(
        [first * cosine - second * sine, second * cosine + first * sine], axis=-1
    )


def unit_rows(vectors, row_gain):
    return (
        vectors * lax.rsqrt(jnp.mean(vectors * vectors, axis=-1, keepdims=True) + 1e-06) * row_gain
    )


def ready_to_store(plain_keys, angle, key_gain):
    wide_keys = plain_keys.astype(jnp.float32)
    wide_keys = unit_rows(wide_keys, key_gain)
    return apply_rotary(wide_keys, angle)


def body(key_rows, value_rows, turn_angle, key_gain):
    moved_keys, stored_values = (
        lax.all_to_all(key_rows, ("block", "span"), split_axis=0, concat_axis=1, tiled=True),
        lax.all_to_all(value_rows, ("block", "span"), split_axis=0, concat_axis=1, tiled=True),
    )
    turned_keys = ready_to_store(moved_keys, turn_angle, key_gain)
    key_scale = jnp.max(jnp.abs(turned_keys), axis=1)
    narrow_keys = (turned_keys / key_scale[:, None]).astype(jnp.bfloat16)
    stored_keys = jnp.transpose(narrow_keys, (0, 2, 3, 1))
    return (stored_keys, stored_values, key_scale)


def solution(mesh):
    return jax.shard_map(
        body,
        mesh=mesh,
        in_specs=(
            P(None, ("block", "span"), "group", None),
            P(None, ("block", "span"), "group", None),
            P(),
            P(),
        ),
        out_specs=(
            P(("block", "span"), "group", None, None),
            P(("block", "span"), None, "group", None),
            P(("block", "span"), "group", None),
        ),
        check_vma=False,
    )
```

profile of v0, /device:TPU:24, one launch (start us, length us, event | category | flops | bytes accessed | tf_op | source)
XLA Modules:
  0.0 291.1 jit_solution(8993941025969121978)
XLA Ops:
  0.6 0.0 copy-start
  0.6 6.4 %all-to-all-start = ((bf16[8,1536,2,128]{3,2,1,0:T(2,128)(2,1)}), bf16[8,1536,2,128]{3,2,1,0:T(2,128)(2,1)}, u32[]{:S(2)}, u32[]{:S(2)}) async-start(bf16[8,1536,2,128]{3,2,1,0:T(2,128)(2,1)} %param.4), calls=%async_computation | async-start | bytes 12582912 | tf_op jit(solution)/shard_map/all_to_all | solution.py:30
  7.0 0.0 copy-done
  7.0 12.2 %fusion.1 = (f32[12288,64]{0,1:T(8,128)}, f32[12288,64]{0,1:T(8,128)}) fusion(f32[12288,64]{0,1:T(8,128)S(1)} %copy-done), kind=kLoop, calls=%fused_computation.9 | loop fusion | bytes 9437184 | tf_op jit(solution)/shard_map/cos | solution.py:9
  19.2 123.2 %all-to-all-done = bf16[8,1536,2,128]{3,2,1,0:T(2,128)(2,1)} async-done(((bf16[8,1536,2,128]{3,2,1,0:T(2,128)(2,1)}), bf16[8,1536,2,128]{3,2,1,0:T(2,128)(2,1)}, u32[]{:S(2)}, u32[]{:S(2)}) %all-to-all-start) | async-done | bytes 6291488 | tf_op jit(solution)/shard_map/all_to_all | solution.py:30
  142.4 6.3 %all-to-all-start.1 = ((bf16[8,1536,2,128]{3,2,1,0:T(2,128)(2,1)}), bf16[8,1536,2,128]{3,2,1,0:T(2,128)(2,1)}, u32[]{:S(2)}, u32[]{:S(2)}) async-start(bf16[8,1536,2,128]{3,2,1,0:T(2,128)(2,1)} %param.5), calls=%async_computation.1 | async-start | bytes 12582912 | tf_op jit(solution)/shard_map/all_to_all | solution.py:31
  148.7 23.2 %multiply_reduce_fusion = f32[8,1536,2]{2,1,0:T(8,128)} fusion(bf16[8,1536,2,128]{3,2,1,0:T(2,128)(2,1)} %all-to-all-done), kind=kLoop, calls=%fused_computation.4 | loop fusion | flops 9412608 | bytes 6389760 | tf_op jit(solution)/shard_map/reduce_sum | solution.py:18
  171.9 6.3 %add_rsqrt_fusion = f32[8,1536,2]{2,1,0:T(8,128)} fusion(f32[8,1536,2]{2,1,0:T(8,128)} %multiply_reduce_fusion), kind=kLoop, calls=%fused_computation.7 | loop fusion | flops 49152 | bytes 196608 | tf_op jit(solution)/shard_map/rsqrt | solution.py:18
  178.2 4.4 %copy.9 = f32[12288,2]{0,1:T(2,128)S(1)} copy(f32[12288,2]{1,0:T(8,128)} %bitcast.7) | data formatting | bytes 196608 | tf_op jit(solution)/shard_map/rsqrt | solution.py:18
  182.6 0.0 copy-start.2
  182.6 17.8 %copy.10 = f32[1,12288,2,128]{1,3,2,0:T(8,128)} copy(bf16[1,12288,2,128]{3,2,1,0:T(2,128)(2,1)} %bitcast.6) | data formatting | bytes 18874368 | tf_op jit(solution)/shard_map/convert_element_type | solution.py:23
  200.4 0.0 copy-done.2
  200.4 11.0 %multiply_multiply_fusion = f32[1,12288,2,128]{1,3,2,0:T(8,128)} fusion(f32[1,12288,2,128]{1,3,2,0:T(8,128)} %copy.10, f32[128]{0:T(128)S(1)} %copy-done.2, f32[12288,2]{0,1:T(2,128)S(1)} %copy.9), kind=kLoop, calls=%fused_computation.3 | loop fusion | flops 6291456 | bytes 25264640 | tf_op jit(solution)/shard_map/mul | solution.py:18
  211.4 9.9 %multiply_subtract_fusion = (f32[1,12288,2,64]{1,3,2,0:T(8,128)S(1)}, f32[1,12288,2,64]{1,3,2,0:T(8,128)}) fusion(f32[1,12288,2,128]{1,3,2,0:T(8,128)} %multiply_multiply_fusion, f32[12288,64]{0,1:T(8,128)} %get-tuple-element.6, f32[12288,64]{0,1:T(8,128)} %get-tuple-element.5), kind=kLoop, calls=%fused_computation.6 | loop fusion | flops 9437184 | bytes 31457280 | tf_op jit(solution)/shard_map/sub | solution.py:12
  221.3 4.0 %abs_reduce_fusion = f32[2,128]{1,0:T(2,128)S(1)} fusion(f32[1,12288,2,64]{1,3,2,0:T(8,128)} %get-tuple-element.4, f32[1,12288,2,64]{1,3,2,0:T(8,128)S(1)} %get-tuple-element.3), kind=kLoop, calls=%fused_computation.2 | loop fusion | flops 9436928 | bytes 12583936 | tf_op jit(solution)/shard_map/reduce_max | solution.py:34
  225.3 0.0 copy-start.1
  225.3 7.0 %fusion = bf16[1,2,128,12288]{3,2,1,0:T(8,128)(2,1)} fusion(f32[2,128]{1,0:T(2,128)S(1)} %abs_reduce_fusion, f32[1,12288,2,64]{1,3,2,0:T(8,128)} %get-tuple-element.4, f32[1,12288,2,64]{1,3,2,0:T(8,128)S(1)} %get-tuple-element.3), kind=kLoop, calls=%fused_computation.8 | loop fusion | flops 9437184 | bytes 18875392 | tf_op jit(solution)/shard_map/transpose | solution.py:36
  232.3 0.0 copy-done.1
  232.3 52.1 %all-to-all-done.1 = bf16[8,1536,2,128]{3,2,1,0:T(2,128)(2,1)} async-done(((bf16[8,1536,2,128]{3,2,1,0:T(2,128)(2,1)}), bf16[8,1536,2,128]{3,2,1,0:T(2,128)(2,1)}, u32[]{:S(2)}, u32[]{:S(2)}) %all-to-all-start.1) | async-done | bytes 6291488 | tf_op jit(solution)/shard_map/all_to_all | solution.py:31
  284.4 6.7 %copy.12 = bf16[1,12288,2,128]{3,2,1,0:T(2,128)(2,1)} copy(bf16[1,12288,2,128]{3,2,1,0:T(2,128)(2,1)} %bitcast.3) | data formatting | bytes 12582912
Async XLA Ops:
  0.6 6.4 %copy-start = (f32[12288,64]{0,1:T(8,128)S(1)}, f32[12288,64]{0,1:T(8,128)}, u32[]{:S(2)}) copy-start(f32[12288,64]{0,1:T(8,128)} %param.6) | copy-start | bytes 9437188
  0.6 141.8 %all-to-all-start = ((bf16[8,1536,2,128]{3,2,1,0:T(2,128)(2,1)}), bf16[8,1536,2,128]{3,2,1,0:T(2,128)(2,1)}, u32[]{:S(2)}, u32[]{:S(2)}) async-start(bf16[8,1536,2,128]{3,2,1,0:T(2,128)(2,1)} %param.4), calls=%async_computation | async-start | bytes 12582912 | tf_op jit(solution)/shard_map/all_to_all | solution.py:30
  142.4 142.0 %all-to-all-start.1 = ((bf16[8,1536,2,128]{3,2,1,0:T(2,128)(2,1)}), bf16[8,1536,2,128]{3,2,1,0:T(2,128)(2,1)}, u32[]{:S(2)}, u32[]{:S(2)}) async-start(bf16[8,1536,2,128]{3,2,1,0:T(2,128)(2,1)} %param.5), calls=%async_computation.1 | async-start | bytes 12582912 | tf_op jit(solution)/shard_map/all_to_all | solution.py:31
  182.6 17.8 %copy-start.2 = (f32[128]{0:T(128)S(1)}, f32[128]{0:T(128)}, u32[]{:S(2)}) copy-start(f32[128]{0:T(128)} %param.7) | copy-start | bytes 1540
  225.3 7.0 %copy-start.1 = (f32[2,128]{1,0:T(2,128)}, f32[2,128]{1,0:T(2,128)S(1)}, u32[]{:S(2)}) copy-start(f32[2,128]{1,0:T(2,128)S(1)} %abs_reduce_fusion) | copy-start | bytes 3076
where the time goes:
time: 296 us; the launch traced here: 291 us
  waiting for transfers between devices  175 us (59%)
  other arithmetic  61.4 us (21%)
  local copies, waits for them, and re-layouts  41.1 us (14%)
  starting transfers between devices  12.6 us (4%)
    all_to_all x1, waiting for transfers between devices, body(): lax.all_to_all(key_rows, ('block', 'span'), split_axis=0, concat_axis=1,...  123 us
    all_to_all x1, waiting for transfers between devices, body(): lax.all_to_all(value_rows, ('block', 'span'), split_axis=0, concat_axis=1...  52.1 us
    reduce_sum x1, other arithmetic, unit_rows(): jnp.mean(vectors * vectors, axis=-1, keepdims=True) + 1e-06  23.2 us
    convert_element_type x1, local copies, waits for them, and re-layouts, ready_to_store(): wide_keys = plain_keys.astype(jnp.float32)  17.8 us
    cos x1, local copies, waits for them, and re-layouts, apply_rotary(): jnp.cos(angle)[None, :, None, :]  12.2 us
    mul x1, other arithmetic, unit_rows(): vectors * lax.rsqrt(jnp.mean(vectors * vectors, axis=-1, keepdims=True) +...  11 us
    sub x1, other arithmetic, apply_rotary(): first * cosine - second * sine  9.86 us
    transpose x1, other arithmetic, body(): stored_keys = jnp.transpose(narrow_keys, (0, 2, 3, 1))  7.03 us
  transfers between devices with their start and end apart: 2, of which 2 were waited for; matrix products, arithmetic and copies ran while one was open for 33% of the time, Pallas kernels for 0%

commit v1 on v0

v1 whole, which is shorter than its diff:
```python
import functools

import jax
import jax.numpy as jnp
from jax import lax
from jax.experimental import pallas as pl
from jax.experimental.pallas import tpu as pltpu
from jax.sharding import PartitionSpec as P

MESH = pl.DeviceIdType.MESH
ANY = pltpu.MemorySpace.HBM
TILE = 128
EPS = 1e-06


def flip(index, offset, size):
    out, width = 0, 1
    while width < size:
        out = out + ((index // width) % 2 + (offset // width) % 2) % 2 * width
        width *= 2
    return out


def sin_cos(angle):
    h = angle * 0.5
    q = h * h
    s = 1.0 / 6227020800.0
    for c in (-1.0 / 39916800, 1.0 / 362880, -1.0 / 5040, 1.0 / 120, -1.0 / 6, 1.0):
        s = s * q + c
    s = s * h
    k = -1.0 / 87178291200.0
    for c in (1.0 / 479001600, -1.0 / 3628800, 1.0 / 40320, -1.0 / 720, 1.0 / 24, -0.5, 1.0):
        k = k * q + c
    return 2.0 * s * k, 1.0 - 2.0 * s * s


def exchange(
    nb, ns, ng, heads,
    key_ref, value_ref, angle_ref, gain_ref,
    okey_ref, ovalue_ref, scale_ref,
    kbuf, relay, turned, angles, gains, peak, wide, own,
    send_sem, recv_sem, hop_send, hop_recv, fwd_send, fwd_recv, local_sem,
):
    n, rows = key_ref.shape[0], key_ref.shape[1]
    places = rows // heads
    half = (rows // 2) // (TILE * heads) * (TILE * heads)
    rest = rows - half
    size = wide.shape[1]
    mid = size // 2
    b, s, g = (lax.axis_index(a) for a in ("block", "span", "group"))
    me = b * ns + s
    low = ng // 2
    line = b * 2 + g // low

    def peer(d, b=b, s=s):
        return (b + d // ns) % nb, flip(s, d % ns, ns)

    def shifted(step):
        at = (line + step) % (2 * nb)
        return at // 2, (at % 2) * low + g % low

    down, up = shifted(2 * nb - 1), shifted(1)
    far = [d for d in range(ns, n)]
    near = [d for d in range(1, ns)]

    bar = pltpu.get_barrier_semaphore()
    for d in near + far:
        pb, ps = peer(d)
        pl.semaphore_signal(bar, inc=1, device_id=(pb, ps, g), device_id_type=MESH)
    for e in range(ns):
        pl.semaphore_signal(bar, inc=1, device_id=(up[0], flip(s, e, ns), up[1]), device_id_type=MESH)
    pl.semaphore_wait(bar, n - 1 + ns)

    sources = (key_ref, value_ref)
    sinks = (kbuf, ovalue_ref)

    def direct(a, d):
        pb, ps = peer(d)
        r = pb * ns + ps
        part = pl.ds(0, rows) if d < ns else pl.ds(0, half)
        return pltpu.make_async_remote_copy(
            src_ref=sources[a].at[r, part], dst_ref=sinks[a].at[me, part],
            send_sem=send_sem.at[a, d], recv_sem=recv_sem.at[a, d],
            device_id=(pb, ps, g), device_id_type=MESH,
        )

    def hop(a, d):
        pb, ps = peer(d)
        r = pb * ns + ps
        return pltpu.make_async_remote_copy(
            src_ref=sources[a].at[r, pl.ds(half, rest)], dst_ref=relay.at[a, d - ns],
            send_sem=hop_send.at[a, d], recv_sem=hop_recv.at[a, d],
            device_id=(down[0], s, down[1]), device_id_type=MESH,
        )

    def forward(a, d):
        owner = up[0] * ns + s
        pb, ps = peer(d, up[0], s)
        return pltpu.make_async_remote_copy(
            src_ref=relay.at[a, d - ns], dst_ref=sinks[a].at[owner, pl.ds(half, rest)],
            send_sem=fwd_send.at[a, d], recv_sem=fwd_recv.at[a, d],
            device_id=(pb, ps, up[1]), device_id_type=MESH,
        )

    for d in far:
        hop(0, d).start()
    order = []
    for i in range(max(len(near), len(far))):
        order += far[i:i + 1] + near[i:i + 1]
    for d in order:
        direct(0, d).start()
    load_angle = pltpu.make_async_copy(angle_ref, angles, local_sem.at[0])
    load_angle.start()
    load_key = pltpu.make_async_copy(key_ref.at[me], kbuf.at[me], local_sem.at[1])
    load_key.start()
    load_value = pltpu.make_async_copy(value_ref.at[me], own, local_sem.at[2])
    load_value.start()
    for d in order:
        direct(1, d).start()

    gains[...] = jnp.broadcast_to(gain_ref[...], (size, size)).T
    peak[...] = jnp.zeros_like(peak)

    def turn(r, first, count):
        def tile(i, carry):
            at = first + i * TILE
            wide[...] = kbuf[r, pl.ds(pl.multiple_of(at * heads, TILE * heads), TILE * heads), :].astype(jnp.float32)
            cols = pl.ds(pl.multiple_of(r * places + at, TILE), TILE)
            sine, cosine = sin_cos(angles[:, cols])
            for h in range(heads):
                x = wide[pl.ds(h, TILE, stride=heads), :].T
                norm = lax.rsqrt(jnp.mean(x * x, axis=0, keepdims=True) + EPS)
                x = x * norm * gains[...]
                lo, hi = x[:mid], x[mid:]
                lo, hi = lo * cosine - hi * sine, hi * cosine + lo * sine
                turned[h, :mid, cols] = lo
                turned[h, mid:, cols] = hi
                peak[h, :mid] = jnp.maximum(peak[h, :mid], jnp.abs(lo))
                peak[h, mid:] = jnp.maximum(peak[h, mid:], jnp.abs(hi))
            return carry

        lax.fori_loop(0, count // TILE, tile, 0)

    def rank(d):
        pb, ps = peer(d)
        return pb * ns + ps

    load_angle.wait()
    load_key.wait()
    turn(me, 0, places)
    load_value.wait()
    store_value = pltpu.make_async_copy(own, ovalue_ref.at[me], local_sem.at[3])
    store_value.start()
    for i in range(max(len(near), len(far))):
        if i < len(far):
            hop(0, far[i]).wait_recv()
            forward(0, far[i]).start()
            hop(1, far[i]).start()
        if i < len(near):
            direct(0, near[i]).wait_recv()
            turn(rank(near[i]), 0, places)
    for d in far:
        direct(0, d).wait_recv()
        turn(rank(d), 0, half // heads)
        hop(1, d).wait_recv()
        forward(1, d).start()
        forward(0, d).wait_recv()
        turn(rank(d), half // heads, rest // heads)

    for h in range(heads):
        scale_ref[h:h + 1, :] = jnp.max(peak[h].T, axis=0, keepdims=True)
        inverse = 1.0 / jnp.max(peak[h], axis=1, keepdims=True)

        def narrow(i, carry):
            cols = pl.ds(pl.multiple_of(i * 4 * TILE, 4 * TILE), 4 * TILE)
            okey_ref[h, :, cols] = (turned[h, :, cols] * inverse).astype(okey_ref.dtype)
            return carry

        lax.fori_loop(0, n * places // (4 * TILE), narrow, 0)

    for d in near + far:
        direct(1, d).wait_recv()
    for d in far:
        forward(1, d).wait_recv()
    for a in range(2):
        for d in near + far:
            direct(a, d).wait_send()
        for d in far:
            hop(a, d).wait_send()
            forward(a, d).wait_send()
    store_value.wait()


def settle(keys_in, values_in, keys_out, values_out):
    keys_out[...] = keys_in[...]
    values_out[...] = values_in[...]


def body(nb, ns, ng, key_rows, value_rows, turn_angle, key_gain):
    n, places, heads, size = key_rows.shape
    rows = places * heads
    length = n * places
    rest = rows - (rows // 2) // (TILE * heads) * (TILE * heads)
    bf16, f32 = jnp.bfloat16, jnp.float32
    dma = pltpu.SemaphoreType.DMA
    whole = pl.BlockSpec(memory_space=pltpu.VMEM)
    hbm = pl.BlockSpec(memory_space=ANY)
    keys, values, scale = pl.pallas_call(
        functools.partial(exchange, nb, ns, ng, heads),
        out_shape=(
            jax.ShapeDtypeStruct((heads, size, length), bf16),
            jax.ShapeDtypeStruct((n, rows, size), bf16),
            jax.ShapeDtypeStruct((heads, size), f32),
        ),
        in_specs=[hbm, hbm, hbm, whole],
        out_specs=(whole, hbm, whole),
        scratch_shapes=[
            pltpu.VMEM((n, rows, size), bf16),
            pltpu.VMEM((2, n - ns, rest, size), bf16),
            pltpu.VMEM((heads, size, length), f32),
            pltpu.VMEM((size // 2, length), f32),
            pltpu.VMEM((size, size), f32),
            pltpu.VMEM((heads, size, TILE), f32),
            pltpu.VMEM((TILE * heads, size), f32),
            pltpu.VMEM((rows, size), bf16),
            dma((2, n)), dma((2, n)), dma((2, n)), dma((2, n)), dma((2, n)), dma((2, n)), dma((4,)),
        ],
        compiler_params=pltpu.CompilerParams(
            collective_id=0, has_side_effects=True, vmem_limit_bytes=60 * 1024 * 1024
        ),
    )(
        key_rows.reshape(n, rows, size),
        value_rows.reshape(n, rows, size),
        turn_angle.T,
        key_gain.reshape(1, size),
    )
    key_block = pl.BlockSpec((heads, size // n, length), lambda i: (0, i, 0))
    value_block = pl.BlockSpec((1, rows, size), lambda i: (i, 0, 0))
    keys, values = pl.pallas_call(
        settle,
        grid=(n,),
        out_shape=(
            jax.ShapeDtypeStruct(keys.shape, bf16),
            jax.ShapeDtypeStruct(values.shape, bf16),
        ),
        in_specs=[key_block, value_block],
        out_specs=(key_block, value_block),
    )(keys, values)
    return keys[None], values.reshape(1, length, heads, size), scale[None]


def solution(mesh):
    nb, ns, ng = (mesh.shape[a] for a in ("block", "span", "group"))
    return jax.shard_map(
        functools.partial(body, nb, ns, ng),
        mesh=mesh,
        in_specs=(
            P(None, ("block", "span"), "group", None),
            P(None, ("block", "span"), "group", None),
            P(),
            P(),
        ),
        out_specs=(
            P(("block", "span"), "group", None, None),
            P(("block", "span"), None, "group", None),
            P(("block", "span"), "group", None),
        ),
        check_vma=False,
    )
```

time: 296 us -> 292 us (0.986); the launches traced: 291 us -> 292 us
  Pallas kernels: 0 us -> 291 us
  waiting for transfers between devices: 175 us -> 0 us
  other arithmetic: 61.4 us -> 0 us
  local copies, waits for them, and re-layouts: 41.1 us -> 0.57 us
  starting transfers between devices: 12.6 us -> 0 us
    pallas_call x0 -> x2, Pallas kernels: none -> 291 us  [the longest x1 279 us: body(): pl.pallas_call(functools.partial(exchange, nb, ns, ng, heads), out_shape=...]
    all_to_all x2 -> x0, waiting for transfers between devices: 175 us -> none  [the longest x1 123 us: body(): lax.all_to_all(key_rows, ('block', 'span'), split_axis=0, concat_axis=1,...]
    reduce_sum x1 -> x0, other arithmetic: 23.2 us -> none  [unit_rows(): jnp.mean(vectors * vectors, axis=-1, keepdims=True) + 1e-06]
    convert_element_type x1 -> x0, local copies, waits for them, and re-layouts: 17.8 us -> none  [ready_to_store(): wide_keys = plain_keys.astype(jnp.float32)]
    all_to_all x2 -> x0, starting transfers between devices: 12.6 us -> none  [the longest x1 6.36 us: body(): lax.all_to_all(key_rows, ('block', 'span'), split_axis=0, concat_axis=1,...]
    cos x1 -> x0, local copies, waits for them, and re-layouts: 12.2 us -> none  [apply_rotary(): jnp.cos(angle)[None, :, None, :]]
    mul x1 -> x0, other arithmetic: 11 us -> none  [unit_rows(): vectors * lax.rsqrt(jnp.mean(vectors * vectors, axis=-1, keepdims=True) +...]
    sub x1 -> x0, other arithmetic: 9.86 us -> none  [apply_rotary(): first * cosine - second * sine]
  transfers between devices with their start and end apart: 2 -> 0, of which waited for: 2 -> 0; matrix products, arithmetic and copies ran while one was open for 33% -> 0% of each run, Pallas kernels for 0% -> 0%
where the time goes in v1:
time: 292 us
  Pallas kernels  291 us (100%)
    pallas_call x1, Pallas kernels, body(): pl.pallas_call(functools.partial(exchange, nb, ns, ng, heads), out_shape=...  279 us
    pallas_call x1, Pallas kernels, body(): pl.pallas_call(settle, grid=(n,), out_shape=(jax.ShapeDtypeStruct(keys.sh...  11.3 us

profile of v1, /device:TPU:24, one launch (start us, length us, event | category | flops | bytes accessed | tf_op | source)
XLA Modules:
  0.0 291.9 jit_solution(16584932030017235904)
XLA Ops:
  0.6 279.5 %shard_map.67 = (bf16[2,128,12288]{2,1,0:T(8,128)(2,1)}, bf16[8,3072,128]{2,1,0:T(8,128)(2,1)}, f32[2,128]{1,0:T(2,128)}) custom-call(bf16[8,3072,128]{2,1,0:T(8,128)(2,1)} %bitcast.7, bf16[8,3072,128]{2,1,0:T(8,128)(2,1)} %bitcast.8, f32[64,12288]{1,0:T(8,128)} %bitcast.9, f32[1,128]{1,0:T(1,128)} %bitcast.11), custom_call_target="tpu_custom_call" | custom-call | tf_op jit(solution)/shard_map/pallas_call | solution.py:208
  280.1 0.0 copy-start
  280.1 11.3 %shard_map.68 = (bf16[2,128,12288]{2,1,0:T(8,128)(2,1)}, bf16[8,3072,128]{2,1,0:T(8,128)(2,1)}) custom-call(bf16[2,128,12288]{2,1,0:T(8,128)(2,1)} %get-tuple-element.8.keys_in, bf16[8,3072,128]{2,1,0:T(8,128)(2,1)} %get-tuple-element.9.values_in), custom_call_target="tpu_custom_call" | custom-call | tf_op jit(solution)/shard_map/pallas_call | solution.py:239
  291.4 0.0 copy-done
  291.4 0.6 copy.8
Async XLA Ops:
  280.1 11.3 %copy-start = (f32[2,128]{1,0:T(2,128)S(1)}, f32[2,128]{1,0:T(2,128)}, u32[]{:S(2)}) copy-start(f32[2,128]{1,0:T(2,128)} %get-tuple-element.12) | copy-start | bytes 3076

commit v2 on v1

v2 whole, which is shorter than its diff:
```python
import functools

import jax
import jax.numpy as jnp
from jax import lax
from jax.experimental import pallas as pl
from jax.experimental.pallas import tpu as pltpu
from jax.sharding import PartitionSpec as P

MESH = pl.DeviceIdType.MESH
ANY = pltpu.MemorySpace.HBM
TILE = 128
EPS = 1e-06


def flip(index, offset, size):
    out, width = 0, 1
    while width < size:
        out = out + ((index // width) % 2 + (offset // width) % 2) % 2 * width
        width *= 2
    return out


def sin_cos(angle):
    h = angle * 0.5
    q = h * h
    s = 1.0 / 6227020800.0
    for c in (-1.0 / 39916800, 1.0 / 362880, -1.0 / 5040, 1.0 / 120, -1.0 / 6, 1.0):
        s = s * q + c
    s = s * h
    k = -1.0 / 87178291200.0
    for c in (1.0 / 479001600, -1.0 / 3628800, 1.0 / 40320, -1.0 / 720, 1.0 / 24, -0.5, 1.0):
        k = k * q + c
    return 2.0 * s * k, 1.0 - 2.0 * s * s


def exchange(
    nb, ns, ng, heads,
    key_ref, value_ref, angle_ref, gain_ref,
    okey_ref, ovalue_ref, scale_ref,
    kbuf, turned, angles, gains, peak, wide,
    send_sem, recv_sem, local_sem,
):
    n, rows = key_ref.shape[0], key_ref.shape[1]
    places = rows // heads
    size = wide.shape[1]
    mid = size // 2
    b, s, g = (lax.axis_index(a) for a in ("block", "span", "group"))
    me = b * ns + s

    def peer(d):
        return (b + d // ns) % nb, flip(s, d % ns, ns)

    far = [d for d in range(ns, n)]
    near = [d for d in range(1, ns)]

    bar = pltpu.get_barrier_semaphore()
    for d in near + far:
        pb, ps = peer(d)
        pl.semaphore_signal(bar, inc=1, device_id=(pb, ps, g), device_id_type=MESH)
    pl.semaphore_wait(bar, n - 1)

    sources = (key_ref, value_ref)
    sinks = (kbuf, ovalue_ref)

    def direct(a, d):
        pb, ps = peer(d)
        r = pb * ns + ps
        return pltpu.make_async_remote_copy(
            src_ref=sources[a].at[r], dst_ref=sinks[a].at[me],
            send_sem=send_sem.at[a, d], recv_sem=recv_sem.at[a, d],
            device_id=(pb, ps, g), device_id_type=MESH,
        )

    order = []
    for i in range(max(len(near), len(far))):
        order += far[i:i + 1] + near[i:i + 1]
    for d in order:
        direct(0, d).start()
    load_angle = pltpu.make_async_copy(angle_ref, angles, local_sem.at[0])
    load_angle.start()
    load_key = pltpu.make_async_copy(key_ref.at[me], kbuf.at[me], local_sem.at[1])
    load_key.start()
    load_value = pltpu.make_async_copy(value_ref.at[me], ovalue_ref.at[me], local_sem.at[2])
    load_value.start()
    for d in order:
        direct(1, d).start()

    gains[...] = jnp.broadcast_to(gain_ref[...], (size, size)).T
    peak[...] = jnp.zeros_like(peak)

    def turn(r, first, count):
        def tile(i, carry):
            at = first + i * TILE
            wide[...] = kbuf[r, pl.ds(pl.multiple_of(at * heads, TILE * heads), TILE * heads), :].astype(jnp.float32)
            cols = pl.ds(pl.multiple_of(r * places + at, TILE), TILE)
            sine, cosine = sin_cos(angles[:, cols])
            for h in range(heads):
                x = wide[pl.ds(h, TILE, stride=heads), :].T
                norm = lax.rsqrt(jnp.mean(x * x, axis=0, keepdims=True) + EPS)
                x = x * norm * gains[...]
                lo, hi = x[:mid], x[mid:]
                lo, hi = lo * cosine - hi * sine, hi * cosine + lo * sine
                turned[h, :mid, cols] = lo
                turned[h, mid:, cols] = hi
                peak[h, :mid] = jnp.maximum(peak[h, :mid], jnp.abs(lo))
                peak[h, mid:] = jnp.maximum(peak[h, mid:], jnp.abs(hi))
            return carry

        lax.fori_loop(0, count // TILE, tile, 0)

    def rank(d):
        pb, ps = peer(d)
        return pb * ns + ps

    load_angle.wait()
    load_key.wait()
    turn(me, 0, places)
    for d in order:
        direct(0, d).wait_recv()
        turn(rank(d), 0, places)

    for h in range(heads):
        scale_ref[h:h + 1, :] = jnp.max(peak[h].T, axis=0, keepdims=True)
        inverse = 1.0 / jnp.max(peak[h], axis=1, keepdims=True)

        def narrow(i, carry):
            cols = pl.ds(pl.multiple_of(i * 4 * TILE, 4 * TILE), 4 * TILE)
            okey_ref[h, :, cols] = (turned[h, :, cols] * inverse).astype(okey_ref.dtype)
            return carry

        lax.fori_loop(0, n * places // (4 * TILE), narrow, 0)

    for d in order:
        direct(1, d).wait_recv()
    for d in order:
        direct(0, d).wait_send()
        direct(1, d).wait_send()
    load_value.wait()


def settle(keys_in, values_in, scale_in, keys_out, values_out, scale_out, sem):
    copies = [
        pltpu.make_async_copy(keys_in, keys_out, sem.at[0]),
        pltpu.make_async_copy(values_in, values_out, sem.at[1]),
        pltpu.make_async_copy(scale_in, scale_out, sem.at[2]),
    ]
    for copy in copies:
        copy.start()
    for copy in copies:
        copy.wait()


def body(nb, ns, ng, key_rows, value_rows, turn_angle, key_gain):
    n, places, heads, size = key_rows.shape
    rows = places * heads
    length = n * places
    bf16, f32 = jnp.bfloat16, jnp.float32
    dma = pltpu.SemaphoreType.DMA
    whole = pl.BlockSpec(memory_space=pltpu.VMEM)
    hbm = pl.BlockSpec(memory_space=ANY)
    keys, values, scale = pl.pallas_call(
        functools.partial(exchange, nb, ns, ng, heads),
        out_shape=(
            pltpu.VMEM((heads, size, length), bf16),
            pltpu.VMEM((n, rows, size), bf16),
            pltpu.VMEM((heads, size), f32),
        ),
        in_specs=[hbm, hbm, hbm, whole],
        out_specs=(whole, whole, whole),
        scratch_shapes=[
            pltpu.VMEM((n, rows, size), bf16),
            pltpu.VMEM((heads, size, length), f32),
            pltpu.VMEM((size // 2, length), f32),
            pltpu.VMEM((size, size), f32),
            pltpu.VMEM((heads, size, TILE), f32),
            pltpu.VMEM((TILE * heads, size), f32),
            dma((2, n)), dma((2, n)), dma((3,)),
        ],
        compiler_params=pltpu.CompilerParams(
            collective_id=0, has_side_effects=True, vmem_limit_bytes=50 * 1024 * 1024
        ),
    )(
        key_rows.reshape(n, rows, size),
        value_rows.reshape(n, rows, size),
        turn_angle.T,
        key_gain.reshape(1, size),
    )
    keys, values, scale = pl.pallas_call(
        settle,
        out_shape=(
            jax.ShapeDtypeStruct(keys.shape, bf16),
            jax.ShapeDtypeStruct(values.shape, bf16),
            jax.ShapeDtypeStruct(scale.shape, f32),
        ),
        in_specs=[whole, whole, whole],
        out_specs=(hbm, hbm, hbm),
        scratch_shapes=[dma((3,))],
        compiler_params=pltpu.CompilerParams(vmem_limit_bytes=1024 * 1024),
    )(keys, values, scale)
    return keys[None], values.reshape(1, length, heads, size), scale[None]


def solution(mesh):
    nb, ns, ng = (mesh.shape[a] for a in ("block", "span", "group"))
    return jax.shard_map(
        functools.partial(body, nb, ns, ng),
        mesh=mesh,
        in_specs=(
            P(None, ("block", "span"), "group", None),
            P(None, ("block", "span"), "group", None),
            P(),
            P(),
        ),
        out_specs=(
            P(("block", "span"), "group", None, None),
            P(("block", "span"), None, "group", None),
            P(("block", "span"), "group", None),
        ),
        check_vma=False,
    )
```

time: 292 us -> 283 us (0.969)
  Pallas kernels: 291 us -> 281 us
    pallas_call x1, Pallas kernels: 11.3 us -> 4.8 us  [body(): pl.pallas_call(settle, out_shape=(jax.ShapeDtypeStruct(keys.shape, bf16),...]
    pallas_call x1, Pallas kernels: 279 us -> 276 us  [body(): pl.pallas_call(functools.partial(exchange, nb, ns, ng, heads), out_shape=...]
where the time goes in v2:
time: 283 us; the launch traced here: 281 us
  Pallas kernels  281 us (99%)
    pallas_call x1, Pallas kernels, body(): pl.pallas_call(functools.partial(exchange, nb, ns, ng, heads), out_shape=...  276 us

profile of v2, /device:TPU:24, one launch (start us, length us, event | category | flops | bytes accessed | tf_op | source)
XLA Modules:
  0.0 281.4 jit_solution(1450214250893980178)
XLA Ops:
  0.6 276.0 %shard_map.67 = (bf16[2,128,12288]{2,1,0:T(8,128)(2,1)S(1)}, bf16[8,3072,128]{2,1,0:T(8,128)(2,1)S(1)}, f32[2,128]{1,0:T(2,128)S(1)}) custom-call(bf16[8,3072,128]{2,1,0:T(8,128)(2,1)} %bitcast.7, bf16[8,3072,128]{2,1,0:T(8,128)(2,1)} %bitcast.8, f32[64,12288]{1,0:T(8,128)} %bitcast.9, f32[1,128]{1,0:T(1,128)} %bitcast.10), custom_call_target="tpu_custom_call" | custom-call | tf_op jit(solution)/shard_map/pallas_call | solution.py:162
  276.6 4.8 %shard_map.68 = (bf16[2,128,12288]{2,1,0:T(8,128)(2,1)}, bf16[8,3072,128]{2,1,0:T(8,128)(2,1)}, f32[2,128]{1,0:T(2,128)}) custom-call(bf16[2,128,12288]{2,1,0:T(8,128)(2,1)S(1)} %get-tuple-element.9.keys_in, bf16[8,3072,128]{2,1,0:T(8,128)(2,1)S(1)} %get-tuple-element.10.values_in, f32[2,128]{1,0:T(2,128)S(1)} %get-tuple-element.11.scale_in), custom_call_target="tpu_custom_call" | custom-call | tf_op jit(solution)/shard_map/pallas_call | solution.py:189
